TPU v7x, 32 devices: a whole 2x2x4 slice. The times are simulated.
32 devices in a mesh: groups: 2 (over y), cells: 8 (over z, x), side: 2 (over core).
Axes of the slice: x: 2, y: 2, z: 4, core: 2. Of those that a mesh axis runs over, the one named last changes fastest.
Arguments:
- datasets: float32 [2, 2000, 8192], P('side', None, ('groups', 'cells')), parts along dimension 2, may hold values from -6 to 6
- sketch: float32 [64, 8192], P(None, ('groups', 'cells')), parts along dimension 1, may hold values from -6 to 6
Outputs:
- factors: float32 [2, 64, 8192], P('side', None, ('groups', 'cells')), parts along dimension 2
There are 2 independent parts, one for each index of `groups`. A program takes and returns all parts, laid end to end along the dimension named above; each array names one. Nothing has to cross between parts.
All inputs are finite; a program needn't handle non-finite values.
Results may differ from a plain program's by a relative error of at most 0.00009.
Values sent between devices are 32-bit elements; how exact they have to be, the bound alone decides.
A program may use at most 64 MiB of HBM per device.

v0:
```python
import jax
import jax.numpy as jnp
from jax import lax
from jax.sharding import PartitionSpec as P


def from_behind(value, axis, steps):
    count = lax.axis_size(axis)
    initial, last = (max(0, -steps), min(count, count - steps))
    return lax.ppermute(value, axis, [(source, source + steps) for source in range(initial, last)])


def per_device(datasets, sketch):
    high = lax.Precision.HIGHEST
    own_data = datasets[0]
    side_index = lax.axis_index("side")
    cell_count = own_data.shape[1] * lax.axis_size("cells")
    scale = jnp.sqrt(jnp.float32(cell_count))
    partial_value = jnp.dot(sketch, own_data.T, precision=high)
    summed = lax.psum(partial_value, "cells")
    arrived = from_behind(summed, "side", -1)
    panel = jnp.where(side_index == 0, arrived, summed)
    range_rows = jnp.dot(panel, own_data, precision=high)
    gram_part = jnp.dot(range_rows, range_rows.T, precision=high)
    raw_part = jnp.dot(range_rows, own_data.T, precision=high)
    gram, raw_cross = lax.psum((gram_part, raw_part), "cells")
    lower = jnp.linalg.cholesky(gram)
    basis = jax.scipy.linalg.solve_triangular(lower, range_rows, lower=True)
    cross = jax.scipy.linalg.solve_triangular(lower, raw_cross, lower=True)
    received = from_behind(cross, "side", 1)
    projected = jnp.dot(received, own_data, precision=high)
    result = jnp.where(side_index == 0, basis * scale, projected / scale)
    return result[None]


def solution(mesh):
    in_specs = (P("side", None, ("groups", "cells")), P(None, ("groups", "cells")))
    out_specs = P("side", None, ("groups", "cells"))
    return jax.shard_map(
        per_device, mesh=mesh, in_specs=in_specs, out_specs=out_specs, check_vma=False
    )
```

profile of v0, /device:TPU:0, one launch (start us, length us, event | category | flops | bytes accessed | tf_op | source)
XLA Modules:
  0.0 225.7 jit_solution(7290744189002880673)
XLA Ops:
  6.5 0.0 copy-start
  6.5 0.0 all-reduce.3.cloned.1.call-start
  6.5 0.9 copy-done
  7.4 6.7 %fusion.6 = f32[64,2000]{1,0:T(8,128)} fusion(f32[64,512]{1,0:T(8,128)S(1)} %copy-done, f32[1,2000,512]{2,1,0:T(8,128)} %param.2), kind=kOutput, calls=%fused_computation.6 | convolution fusion | flops 786432000 | bytes 4739072 | tf_op jit(solution)/shard_map/dot_general | solution.py:19
  14.1 0.0 all-reduce.3.cloned.1.call-update
  14.2 0.0 all-reduce.5.cloned.1.call-start
  14.2 75.5 %all-reduce.3.cloned.1.call-done = f32[64,2000]{1,0:T(8,128)} async-done(((f32[64,2000]{1,0:T(8,128)}), f32[64,2000]{1,0:T(8,128)}) %all-reduce.3.cloned.1.call-update) | async-done | bytes 512016 | tf_op jit(solution)/shard_map/psum | solution.py:20
  89.7 1.3 collective-permute-start
  91.0 0.0 copy-start.1
  91.0 2.7 %collective-permute-done = f32[64,2000]{1,0:T(8,128)S(1)} collective-permute-done((f32[64,2000]{1,0:T(8,128)}, f32[64,2000]{1,0:T(8,128)S(1)}, u32[]{:S(2)}, u32[]{:S(2)}) %collective-permute-start) | collective-permute-done | bytes 512032 | tf_op jit(solution)/shard_map/ppermute | solution.py:10
  93.7 4.8 %fusion.4 = f32[64,512]{1,0:T(8,128)S(1)} fusion(f32[1,2000,512]{2,1,0:T(8,128)} %param.2, f32[64,2000]{1,0:T(8,128)S(1)} %collective-permute-done, f32[64,2000]{1,0:T(8,128)} %all-reduce.3.cloned.1.call-done, pred[]{:T(512)S(6)} %eq.4), kind=kOutput, calls=%fused_computation.4 | convolution fusion | flops 786560000 | bytes 5251073 | tf_op jit(solution)/shard_map/dot_general | solution.py:23
  98.5 0.3 fusion.24
  98.7 0.0 copy-done.1
  98.7 4.6 %fusion.2 = f32[64,2000]{1,0:T(8,128)} fusion(f32[64,512]{1,0:T(8,128)S(1)} %fusion.4, f32[1,2000,512]{2,1,0:T(8,128)S(1)} %copy-done.1), kind=kOutput, calls=%fused_computation.2 | convolution fusion | flops 786432000 | bytes 4739072 | tf_op jit(solution)/shard_map/dot_general | solution.py:25
  103.3 35.4 %psum.22 = f32[64,64]{0,1:T(8,128)S(1)} all-reduce(f32[64,64]{0,1:T(8,128)S(1)} %fusion.24), channel_id=1, replica_groups=mesh['groups'=2,'cells'=8,'side'=2] {'cells'}, use_global_device_ids=true, to_apply=%region_1.2 | all-reduce | flops 4096 | bytes 32768 | tf_op jit(solution)/shard_map/psum | solution.py:26
  138.7 0.1 copy.4
  138.8 0.0 all-reduce.5.cloned.1.call-update
  138.8 5.8 %cholesky.16 = f32[64,64]{1,0:T(8,128)S(1)} custom-call(f32[64,64]{1,0:T(8,128)S(1)} %fusion.23), custom_call_target="Cholesky" | custom-call | tf_op jit(solution)/shard_map/jit(cholesky)/cholesky | solution.py:27
  144.7 0.6 compare_reduce_fusion
  145.3 0.7 fusion.19
  146.0 4.9 %custom-call.10 = f32[1,64,64]{1,2,0:T(8,128)S(1)} custom-call(f32[1,64,64]{2,1,0:T(8,128)S(1)} %fusion.19), custom_call_target="InvertDiagBlocksLowerTriangular" | custom-call | tf_op jit(solution)/shard_map/jit(_solve_triangular)/triangular_solve | solution.py:28
  150.9 58.1 %all-reduce.5.cloned.1.call-done = f32[64,2000]{1,0:T(8,128)} async-done(((f32[64,2000]{1,0:T(8,128)}), f32[64,2000]{1,0:T(8,128)}) %all-reduce.5.cloned.1.call-update) | async-done | bytes 512016 | tf_op jit(solution)/shard_map/psum | solution.py:26
  209.0 1.7 fusion.20
  210.6 1.3 collective-permute-start.1
  212.0 0.3 convolution_multiply_fusion
  212.3 1.2 collective-permute-done.1
  213.5 5.4 %fusion.14 = f32[1,64,512]{2,1,0:T(8,128)} fusion(f32[64,512]{1,0:T(8,128)S(1)} %convolution_multiply_fusion, f32[64,2000]{1,0:T(8,128)S(1)} %collective-permute-done.1, f32[1,2000,512]{2,1,0:T(8,128)} %param.2, pred[]{:T(512)S(6)} %eq.4), kind=kOutput, calls=%fused_computation.10 | convolution fusion | flops 786497536 | bytes 4870145 | tf_op jit(solution)/shard_map/dot_general | solution.py:31
  (2 shorter events, 0.0 us)
Async XLA Ops:
  6.5 0.9 copy-start
  6.5 83.2 %all-reduce.3.cloned.1.call-start = ((), (), s32[]{:S(2)}) async-start(), calls=%async_computation | async-start | bytes 1048576 | tf_op jit(solution)/shard_map/psum | solution.py:20
  14.2 194.8 %all-reduce.5.cloned.1.call-start = ((), (), s32[]{:S(2)}) async-start(), calls=%async_computation.1 | async-start | bytes 1048576 | tf_op jit(solution)/shard_map/psum | solution.py:26
  89.7 4.0 %collective-permute-start = (f32[64,2000]{1,0:T(8,128)}, f32[64,2000]{1,0:T(8,128)S(1)}, u32[]{:S(2)}, u32[]{:S(2)}) collective-permute-start(f32[64,2000]{1,0:T(8,128)} %all-reduce.3.cloned.1.call-done), channel_id=1, source_target_pairs={{1,0},{3,2},{5,4},{7,6},{9,8},{11,10},{13,12},{15,14},{17,16},{19,... | collective-permute-start | bytes 1536008 | tf_op jit(solution)/shard_map/ppermute | solution.py:10
  91.0 7.7 %copy-start.1 = (f32[1,2000,512]{2,1,0:T(8,128)S(1)}, f32[1,2000,512]{2,1,0:T(8,128)}, u32[]{:S(2)}) copy-start(f32[1,2000,512]{2,1,0:T(8,128)} %param.2) | copy-start | bytes 12288004
  210.6 2.8 %collective-permute-start.1 = (f32[64,2000]{1,0:T(8,128)S(1)}, f32[64,2000]{1,0:T(8,128)S(1)}, u32[]{:S(2)}, u32[]{:S(2)}) collective-permute-start(f32[64,2000]{1,0:T(8,128)S(1)} %fusion.20), channel_id=1, source_target_pairs={{0,1},{2,3},{4,5},{6,7},{8,9},{10,11},{12,13},{14,15},{16,17},{18,... | collective-permute-start | bytes 1536008 | tf_op jit(solution)/shard_map/ppermute | solution.py:10
Sparse Core Ops, SparseCore 0:
  14.3 75.3 all-reduce.2
  138.9 70.0 all-reduce.4
where the time goes:
time: 226 us
  waiting for transfers between devices  137 us (61%)
  blocking collectives  35.4 us (16%)
  matrix products  23.7 us (10%)
  between operations  13.5 us (6%)
  other arithmetic  12.1 us (5%)
  starting transfers between devices  2.65 us (1%)
    psum x1, waiting for transfers between devices, per_device(): summed = lax.psum(partial_value, 'cells')  75.5 us
    psum x1, waiting for transfers between devices, per_device(): gram, raw_cross = lax.psum((gram_part, raw_part), 'cells')  58.1 us
    psum x1, blocking collectives, per_device(): gram, raw_cross = lax.psum((gram_part, raw_part), 'cells')  35.4 us
    dot_general x1, matrix products, per_device(): partial_value = jnp.dot(sketch, own_data.T, precision=high)  6.69 us
    another operation x3, other arithmetic, per_device(): lower = jnp.linalg.cholesky(gram)  6.52 us
    another operation x2, other arithmetic, per_device(): basis = jax.scipy.linalg.solve_triangular(lower, range_rows, lower=True)  5.55 us
    dot_general x1, matrix products, per_device(): projected = jnp.dot(received, own_data, precision=high)  5.43 us
    dot_general x1, matrix products, per_device(): range_rows = jnp.dot(panel, own_data, precision=high)  4.75 us
  transfers between devices with their start and end apart: 4, of which 4 were waited for; matrix products, arithmetic and copies ran while one was open for 5% of the time, Pallas kernels for 0%

commit v1 on v0

--- a/solution.py
+++ b/solution.py
@@ -17,7 +17,9 @@
     cell_count = own_data.shape[1] * lax.axis_size("cells")
     scale = jnp.sqrt(jnp.float32(cell_count))
     partial_value = jnp.dot(sketch, own_data.T, precision=high)
-    summed = lax.psum(partial_value, "cells")
+    summed = partial_value
+    for hop in (1, 2, 4):
+        summed = summed + lax.ppermute(summed, "cells", [(dev, dev ^ hop) for dev in range(8)])
     arrived = from_behind(summed, "side", -1)
     panel = jnp.where(side_index == 0, arrived, summed)
     range_rows = jnp.dot(panel, own_data, precision=high)

time: 226 us -> 204 us (0.903)
  waiting for transfers between devices: 137 us -> 107 us
  starting transfers between devices: 2.65 us -> 10.4 us
    psum x1 -> x0, waiting for transfers between devices: 75.5 us -> none  [per_device(): summed = lax.psum(partial_value, 'cells')]
    ppermute x0 -> x3, waiting for transfers between devices: none -> 45 us  [per_device(): lax.ppermute(summed, 'cells', [(dev, dev ^ hop) for dev in range(8)])]
    ppermute x0 -> x3, starting transfers between devices: none -> 7.56 us  [per_device(): lax.ppermute(summed, 'cells', [(dev, dev ^ hop) for dev in range(8)])]
  transfers between devices with their start and end apart: 4 -> 6, of which waited for: 4 -> 6; matrix products, arithmetic and copies ran while one was open for 5% -> 6% of each run, Pallas kernels for 0% -> 0%
where the time goes in v1:
time: 204 us
  waiting for transfers between devices  107 us (52%)
  blocking collectives  37 us (18%)
  matrix products  22.9 us (11%)
  between operations  13.5 us (7%)
  other arithmetic  12.3 us (6%)
  starting transfers between devices  10.4 us (5%)
    psum x1, waiting for transfers between devices, per_device(): gram, raw_cross = lax.psum((gram_part, raw_part), 'cells')  58.2 us
    ppermute x3, waiting for transfers between devices, per_device(): lax.ppermute(summed, 'cells', [(dev, dev ^ hop) for dev in range(8)])  45 us
    psum x1, blocking collectives, per_device(): gram, raw_cross = lax.psum((gram_part, raw_part), 'cells')  37 us
    ppermute x3, starting transfers between devices, per_device(): lax.ppermute(summed, 'cells', [(dev, dev ^ hop) for dev in range(8)])  7.56 us
    another operation x3, other arithmetic, per_device(): lower = jnp.linalg.cholesky(gram)  6.52 us
    dot_general x1, matrix products, per_device(): partial_value = jnp.dot(sketch, own_data.T, precision=high)  5.88 us
    another operation x2, other arithmetic, per_device(): basis = jax.scipy.linalg.solve_triangular(lower, range_rows, lower=True)  5.55 us
    dot_general x1, matrix products, per_device(): projected = jnp.dot(received, own_data, precision=high)  5.42 us
  transfers between devices with their start and end apart: 6, of which 6 were waited for; matrix products, arithmetic and copies ran while one was open for 6% of the time, Pallas kernels for 0%

profile of v1, /device:TPU:0, one launch (start us, length us, event | category | flops | bytes accessed | tf_op | source)
XLA Modules:
  0.0 203.7 jit_solution(6312519002897353469)
XLA Ops:
  6.5 0.0 copy-start
  6.5 0.0 all-reduce.2.cloned.1.call-start
  6.5 0.9 copy-done
  7.4 5.9 %fusion.6 = f32[64,2000]{1,0:T(8,128)S(1)} fusion(f32[64,512]{1,0:T(8,128)S(1)} %copy-done, f32[1,2000,512]{2,1,0:T(8,128)} %param.2), kind=kOutput, calls=%fused_computation.6 | convolution fusion | flops 786432000 | bytes 4739072 | tf_op jit(solution)/shard_map/dot_general | solution.py:19
  13.3 3.0 %collective-permute-start = (f32[64,2000]{1,0:T(8,128)S(1)}, f32[64,2000]{1,0:T(8,128)S(1)}, u32[]{:S(2)}, u32[]{:S(2)}) collective-permute-start(f32[64,2000]{1,0:T(8,128)S(1)} %fusion.6), channel_id=1, source_target_pairs={{0,2},{2,0},{4,6},{6,4},{8,10},{10,8},{12,14},{14,12},{1,3},{3,1},... | collective-permute-start | bytes 1536008 | tf_op jit(solution)/shard_map/ppermute | solution.py:22
  16.4 11.9 %collective-permute-done = f32[64,2000]{1,0:T(8,128)S(1)} collective-permute-done((f32[64,2000]{1,0:T(8,128)S(1)}, f32[64,2000]{1,0:T(8,128)S(1)}, u32[]{:S(2)}, u32[]{:S(2)}) %collective-permute-start) | collective-permute-done | bytes 512032 | tf_op jit(solution)/shard_map/ppermute | solution.py:22
  28.3 0.1 add.28
  28.3 1.9 collective-permute-start.1
  30.2 11.3 %collective-permute-done.1 = f32[64,2000]{1,0:T(8,128)S(1)} collective-permute-done((f32[64,2000]{1,0:T(8,128)S(1)}, f32[64,2000]{1,0:T(8,128)S(1)}, u32[]{:S(2)}, u32[]{:S(2)}) %collective-permute-start.1) | collective-permute-done | bytes 512032 | tf_op jit(solution)/shard_map/ppermute | solution.py:22
  41.5 0.1 add.29
  41.6 2.6 %collective-permute-start.2 = (f32[64,2000]{1,0:T(8,128)S(1)}, f32[64,2000]{1,0:T(8,128)S(1)}, u32[]{:S(2)}, u32[]{:S(2)}) collective-permute-start(f32[64,2000]{1,0:T(8,128)S(1)} %add.29), channel_id=1, source_target_pairs={{0,8},{2,10},{4,12},{6,14},{8,0},{10,2},{12,4},{14,6},{1,9},{3,11}... | collective-permute-start | bytes 1536008 | tf_op jit(solution)/shard_map/ppermute | solution.py:22
  44.2 21.8 %collective-permute-done.2 = f32[64,2000]{1,0:T(8,128)S(1)} collective-permute-done((f32[64,2000]{1,0:T(8,128)S(1)}, f32[64,2000]{1,0:T(8,128)S(1)}, u32[]{:S(2)}, u32[]{:S(2)}) %collective-permute-start.2) | collective-permute-done | bytes 512032 | tf_op jit(solution)/shard_map/ppermute | solution.py:22
  66.0 0.1 add.30
  66.0 1.3 collective-permute-start.3
  67.3 0.0 copy-start.1
  67.4 2.5 %collective-permute-done.3 = f32[64,2000]{1,0:T(8,128)S(1)} collective-permute-done((f32[64,2000]{1,0:T(8,128)S(1)}, f32[64,2000]{1,0:T(8,128)S(1)}, u32[]{:S(2)}, u32[]{:S(2)}) %collective-permute-start.3) | collective-permute-done | bytes 512032 | tf_op jit(solution)/shard_map/ppermute | solution.py:10
  69.8 4.7 %fusion.4 = f32[64,512]{1,0:T(8,128)S(1)} fusion(f32[1,2000,512]{2,1,0:T(8,128)} %param.2, f32[64,2000]{1,0:T(8,128)S(1)} %collective-permute-done.3, f32[64,2000]{1,0:T(8,128)S(1)} %add.30, pred[]{:T(512)S(6)} %eq.4), kind=kOutput, calls=%fused_computation.4 | convolution fusion | flops 786560000 | bytes 5251073 | tf_op jit(solution)/shard_map/dot_general | solution.py:25
  74.6 0.3 fusion.24
  74.9 0.0 copy-done.1
  74.9 4.6 %fusion.2 = f32[64,2000]{1,0:T(8,128)} fusion(f32[64,512]{1,0:T(8,128)S(1)} %fusion.4, f32[1,2000,512]{2,1,0:T(8,128)S(1)} %copy-done.1), kind=kOutput, calls=%fused_computation.2 | convolution fusion | flops 786432000 | bytes 4739072 | tf_op jit(solution)/shard_map/dot_general | solution.py:27
  79.5 37.0 %psum.14 = f32[64,64]{0,1:T(8,128)S(1)} all-reduce(f32[64,64]{0,1:T(8,128)S(1)} %fusion.24), channel_id=1, replica_groups=mesh['groups'=2,'cells'=8,'side'=2] {'cells'}, use_global_device_ids=true, to_apply=%region_0.1 | all-reduce | flops 4096 | bytes 32768 | tf_op jit(solution)/shard_map/psum | solution.py:28
  116.4 0.1 copy.4
  116.5 0.0 all-reduce.2.cloned.1.call-update
  116.6 5.8 %cholesky.16 = f32[64,64]{1,0:T(8,128)S(1)} custom-call(f32[64,64]{1,0:T(8,128)S(1)} %fusion.23), custom_call_target="Cholesky" | custom-call | tf_op jit(solution)/shard_map/jit(cholesky)/cholesky | solution.py:29
  122.4 0.6 compare_reduce_fusion
  123.1 0.7 fusion.19
  123.7 4.9 %custom-call.10 = f32[1,64,64]{1,2,0:T(8,128)S(1)} custom-call(f32[1,64,64]{2,1,0:T(8,128)S(1)} %fusion.19), custom_call_target="InvertDiagBlocksLowerTriangular" | custom-call | tf_op jit(solution)/shard_map/jit(_solve_triangular)/triangular_solve | solution.py:30
  128.6 58.2 %all-reduce.2.cloned.1.call-done = f32[64,2000]{1,0:T(8,128)} async-done(((f32[64,2000]{1,0:T(8,128)}), f32[64,2000]{1,0:T(8,128)}) %all-reduce.2.cloned.1.call-update) | async-done | bytes 512016 | tf_op jit(solution)/shard_map/psum | solution.py:28
  186.8 1.7 fusion.20
  188.5 1.5 collective-permute-start.4
  190.0 0.3 convolution_multiply_fusion
  190.3 1.2 collective-permute-done.4
  191.5 5.4 %fusion.14 = f32[1,64,512]{2,1,0:T(8,128)} fusion(f32[64,512]{1,0:T(8,128)S(1)} %convolution_multiply_fusion, f32[64,2000]{1,0:T(8,128)S(1)} %collective-permute-done.4, f32[1,2000,512]{2,1,0:T(8,128)} %param.2, pred[]{:T(512)S(6)} %eq.4), kind=kOutput, calls=%fused_computation.10 | convolution fusion | flops 786497536 | bytes 4870145 | tf_op jit(solution)/shard_map/dot_general | solution.py:33
  (2 shorter events, 0.0 us)
Async XLA Ops:
  6.5 0.9 copy-start
  6.5 180.3 %all-reduce.2.cloned.1.call-start = ((), (), s32[]{:S(2)}) async-start(), calls=%async_computation | async-start | bytes 1048576 | tf_op jit(solution)/shard_map/psum | solution.py:28
  13.3 15.0 %collective-permute-start = (f32[64,2000]{1,0:T(8,128)S(1)}, f32[64,2000]{1,0:T(8,128)S(1)}, u32[]{:S(2)}, u32[]{:S(2)}) collective-permute-start(f32[64,2000]{1,0:T(8,128)S(1)} %fusion.6), channel_id=1, source_target_pairs={{0,2},{2,0},{4,6},{6,4},{8,10},{10,8},{12,14},{14,12},{1,3},{3,1},... | collective-permute-start | bytes 1536008 | tf_op jit(solution)/shard_map/ppermute | solution.py:22
  28.3 13.1 %collective-permute-start.1 = (f32[64,2000]{1,0:T(8,128)S(1)}, f32[64,2000]{1,0:T(8,128)S(1)}, u32[]{:S(2)}, u32[]{:S(2)}) collective-permute-start(f32[64,2000]{1,0:T(8,128)S(1)} %add.28), channel_id=1, source_target_pairs={{0,4},{2,6},{4,0},{6,2},{8,12},{10,14},{12,8},{14,10},{1,5},{3,7},... | collective-permute-start | bytes 1536008 | tf_op jit(solution)/shard_map/ppermute | solution.py:22
  41.6 24.4 %collective-permute-start.2 = (f32[64,2000]{1,0:T(8,128)S(1)}, f32[64,2000]{1,0:T(8,128)S(1)}, u32[]{:S(2)}, u32[]{:S(2)}) collective-permute-start(f32[64,2000]{1,0:T(8,128)S(1)} %add.29), channel_id=1, source_target_pairs={{0,8},{2,10},{4,12},{6,14},{8,0},{10,2},{12,4},{14,6},{1,9},{3,11}... | collective-permute-start | bytes 1536008 | tf_op jit(solution)/shard_map/ppermute | solution.py:22
  66.0 3.8 %collective-permute-start.3 = (f32[64,2000]{1,0:T(8,128)S(1)}, f32[64,2000]{1,0:T(8,128)S(1)}, u32[]{:S(2)}, u32[]{:S(2)}) collective-permute-start(f32[64,2000]{1,0:T(8,128)S(1)} %add.30), channel_id=1, source_target_pairs={{1,0},{3,2},{5,4},{7,6},{9,8},{11,10},{13,12},{15,14},{17,16},{19,... | collective-permute-start | bytes 1536008 | tf_op jit(solution)/shard_map/ppermute | solution.py:10
  67.3 7.5 %copy-start.1 = (f32[1,2000,512]{2,1,0:T(8,128)S(1)}, f32[1,2000,512]{2,1,0:T(8,128)}, u32[]{:S(2)}) copy-start(f32[1,2000,512]{2,1,0:T(8,128)} %param.2) | copy-start | bytes 12288004
  188.5 3.0 %collective-permute-start.4 = (f32[64,2000]{1,0:T(8,128)S(1)}, f32[64,2000]{1,0:T(8,128)S(1)}, u32[]{:S(2)}, u32[]{:S(2)}) collective-permute-start(f32[64,2000]{1,0:T(8,128)S(1)} %fusion.20), channel_id=1, source_target_pairs={{0,1},{2,3},{4,5},{6,7},{8,9},{10,11},{12,13},{14,15},{16,17},{18,... | collective-permute-start | bytes 1536008 | tf_op jit(solution)/shard_map/ppermute | solution.py:10
Sparse Core Ops, SparseCore 0:
  116.7 70.0 all-reduce.1
